TPU v7x, 8 devices: a whole 2x2x1 slice. The times are simulated.
8 devices in a mesh: part: 1 (over z), data: 2 (over y), model: 4 (over x, core).
Axes of the slice: x: 2, y: 2, z: 1, core: 2. Of those that a mesh axis runs over, the one named last changes fastest.
Arguments:
- x: bfloat16 [2, 32, 1024, 768], P(None, ('part', 'data'), 'model')
- lengths: int32 [2, 32], P(None, ('part', 'data'))
- norm_gain: bfloat16 [2, 768], P(None, 'data')
- w_in: bfloat16 [2, 768, 6912], P(None, 'data', 'model')
- w_kv: bfloat16 [2, 768, 128], P(None, 'data')
- w_out: bfloat16 [2, 3840, 768], P(None, 'model', 'data')
Outputs:
- output: bfloat16 [2, 32, 1024, 768], P(None, ('part', 'data'), 'model')
All inputs are finite; a program needn't handle non-finite values.
Results may differ from a plain program's by a relative error of at most 0.0131665.
Values are sent between devices in bfloat16 or wider.
A program may use at most 1 GiB of HBM per device.

v0:
```python
import math
import jax
import jax.numpy as jnp
from jax import lax
from jax.sharding import PartitionSpec as P, NamedSharding

NORM_EPS = 1e-6
NEG_BIG = -1e30


def layer_norm(x_act, gain_vec):
    x_f32 = x_act.astype(jnp.float32)
    centered = x_f32 - jnp.mean(x_f32, axis=-1, keepdims=True)
    variance = jnp.mean(centered * centered, axis=-1, keepdims=True)
    return (centered * lax.rsqrt(variance + NORM_EPS) * gain_vec.astype(jnp.float32)).astype(jnp.bfloat16)


def attention(q_heads, k_all, v_all, seq_lens, q_offset):
    q_len = q_heads.shape[1]
    k_len = k_all.shape[1]
    head_dim = k_all.shape[2]
    scores = jnp.einsum("bqhc,bkc->bhqk", q_heads, k_all, preferred_element_type=jnp.float32) * (1.0 / math.sqrt(head_dim))
    q_pos = q_offset + lax.broadcasted_iota(jnp.int32, (q_len, 1), 0)
    k_pos = lax.broadcasted_iota(jnp.int32, (1, k_len), 1)
    allowed = (k_pos <= q_pos)[None, None] & (k_pos[None, None] < seq_lens[:, None, None, None])
    scores = jnp.where(allowed, scores, NEG_BIG)
    attn_probs = jax.nn.softmax(scores, axis=-1).astype(jnp.bfloat16)
    return jnp.einsum("bhqk,bkc->bqhc", attn_probs, v_all, preferred_element_type=jnp.float32).astype(jnp.bfloat16)


def layer_block(x_loc, seq_lens, gain_full, w_in3, w_kv_full, w_out3, n_model):
    n_seqs, t_loc, d_model = x_loc.shape
    head_dim = w_kv_full.shape[1] // 2
    ff_head = (w_in3.shape[2] - head_dim) // 2
    h_loc = layer_norm(x_loc, gain_full)
    h_all = lax.all_gather(h_loc, "model", axis=1, tiled=True)
    projected = jnp.einsum("btd,dhc->bthc", h_all, w_in3, preferred_element_type=jnp.float32).astype(jnp.bfloat16)
    kv_act = jnp.einsum("btd,dc->btc", h_all, w_kv_full, preferred_element_type=jnp.float32).astype(jnp.bfloat16)
    attn_out = attention(projected[..., :head_dim], kv_act[..., :head_dim], kv_act[..., head_dim:], seq_lens, 0)
    gate_act = projected[..., head_dim:head_dim + ff_head]
    up_act = projected[..., head_dim + ff_head:]
    mlp_out = (jax.nn.silu(gate_act.astype(jnp.float32)) * up_act.astype(jnp.float32)).astype(jnp.bfloat16)
    joined = jnp.concatenate([attn_out, mlp_out], axis=-1)
    group_sum = jnp.einsum("bthc,hcd->btd", joined, w_out3, preferred_element_type=jnp.float32).astype(jnp.bfloat16)
    received = lax.all_to_all(group_sum.reshape(n_seqs, n_model, t_loc, d_model), "model", 1, 1, tiled=True)
    z_sum = jnp.sum(received.astype(jnp.float32), axis=1)
    return (x_loc.astype(jnp.float32) + z_sum).astype(jnp.bfloat16)


def solution(mesh):
    n_model = mesh.shape["model"]
    act_spec = P(None, ("part", "data"), "model", None)

    def local_fn(x_blk, len_blk, gain_blk, w_in_blk, w_kv_blk, w_out_blk):
        head_dim = w_kv_blk.shape[2] // 2
        hidden = [x_blk[micro_idx] for micro_idx in range(x_blk.shape[0])]
        for layer_idx in range(gain_blk.shape[0]):
            gain_full = lax.all_gather(gain_blk[layer_idx], "data", axis=0, tiled=True)
            w_in_loc = lax.all_gather(w_in_blk[layer_idx], "data", axis=0, tiled=True)
            w_kv_full = lax.all_gather(w_kv_blk[layer_idx], "data", axis=0, tiled=True)
            w_out_loc = lax.all_gather(w_out_blk[layer_idx], "data", axis=1, tiled=True)
            d_model, in_loc = w_in_loc.shape
            out_loc = w_out_loc.shape[0]
            ff_loc = in_loc - out_loc
            heads_loc = (out_loc - ff_loc) // head_dim
            w_in3 = w_in_loc.reshape(d_model, heads_loc, in_loc // heads_loc)
            w_out3 = w_out_loc.reshape(heads_loc, out_loc // heads_loc, d_model)
            for micro_idx in range(len(hidden)):
                hidden[micro_idx] = layer_block(hidden[micro_idx], len_blk[micro_idx], gain_full, w_in3, w_kv_full, w_out3, n_model)
        return jnp.stack(hidden)

    return jax.shard_map(
        local_fn,
        mesh=mesh,
        in_specs=(act_spec, P(None, ("part", "data")), P(None, "data"), P(None, "data", "model"), P(None, "data", None), P(None, "model", "data")),
        out_specs=act_spec,
        check_vma=False,
    )
```

profile of v0, /device:TPU:0, one launch (start us, length us, event | category | flops | bytes accessed | tf_op | source)
XLA Modules:
  0.0 2389.4 jit_solution(16037643351476092342)
XLA Ops:
  64.0 141.9 %all-gather.21.cloned.1.call-done = bf16[16,1024,768]{2,1,0:T(8,128)(2,1)} async-done(((bf16[16,256,768]{2,1,0:T(8,128)(2,1)}), bf16[16,1024,768]{2,1,0:T(8,128)(2,1)}) %all-gather.21.cloned.1.call-update) | async-done | bytes 25165840 | tf_op jit(solution)/shard_map/all_gather | solution.py:36
  206.0 51.7 %convolution_convert_fusion.1 = bf16[16,1024,3,576]{1,3,2,0:T(8,128)(2,1)} fusion(bf16[768,3,576,1]{0,2,1,3:T(8,128)(2,1)} %bitcast.257, bf16[16,1024,768]{2,1,0:T(8,128)(2,1)} %all-gather.21.cloned.1.call-done), kind=kOutput, calls=%fused_computation.73 | convolution fusion | flops 43514855424 | bytes 84443136 | tf_op jit(solution)/shard_map/btd,dhc->bthc/dot_general | solution.py:37
  275.9 31.5 %fusion.41 = bf16[16,1024,3,256]{1,3,2,0:T(8,128)(2,1)} fusion(bf16[16,1024,3,576]{1,3,2,0:T(8,128)(2,1)} %convolution_convert_fusion.1), kind=kLoop, calls=%fused_computation.69 | loop fusion | flops 100663296 | bytes 75497472 | tf_op jit(solution)/shard_map/convert_element_type | solution.py:42
  307.4 81.7 %fusion.165 = (f32[16,3,1024]{2,1,0:T(4,128)S(1)}, f32[16,3,1024,1024]{2,3,1,0:T(8,128)}) fusion(pred[16,1024,1024]{1,2,0:T(8,128)(4,1)} %get-tuple-element.24, bf16[16,1024,3,576]{1,3,2,0:T(8,128)(2,1)} %convolution_convert_fusion.1, bf16[16,1024,128]{1,2,0:T(8,128)(2,1)} %convolution_convert_fusion.5), kind=kOutput, calls=%fused_computation.209 | convolution fusion | flops 6643778560 | bytes 226689024 | tf_op jit(solution)/shard_map/sub | solution.py:27
  389.1 63.9 %convert_bitcast_fusion.3 = bf16[16,1024,3,64]{1,3,2,0:T(8,128)(2,1)} fusion(f32[16,3,1024,1024]{2,3,1,0:T(8,128)} %get-tuple-element.36, f32[16,3,1024]{2,1,0:T(4,128)S(1)} %get-tuple-element.35, bf16[16,1024,128]{1,2,0:T(8,128)(2,1)} %convolution_convert_fusion.5), kind=kOutput, calls=%fused_computation.146 | convolution fusion | flops 6546259968 | bytes 209911808 | tf_op jit(solution)/shard_map/bhqk,bkc->bqhc/dot_general | solution.py:28
  453.0 33.8 %bitcast_convert_fusion.1 = bf16[16,1024,768]{2,1,0:T(8,128)(2,1)} fusion(bf16[3,320,768,1]{2,1,0,3:T(8,128)(2,1)} %bitcast.261, bf16[16,1024,3,256]{1,3,2,0:T(8,128)(2,1)} %fusion.41, bf16[16,1024,3,64]{1,3,2,0:T(8,128)(2,1)} %convert_bitcast_fusion.3), kind=kOutput, calls=%fused_computation.61 | convolution fusion | flops 24234688512 | bytes 58097664 | tf_op jit(solution)/shard_map/bthc,hcd->btd/dot_general | solution.py:44
  486.8 21.0 copy.13
  516.7 129.8 %convolution_convert_fusion.3 = bf16[16,1024,3,576]{1,3,2,0:T(8,128)(2,1)} fusion(bf16[768,3,576,1]{0,2,1,3:T(8,128)(2,1)S(1)} %bitcast.258, bf16[16,1024,768]{2,1,0:T(8,128)(2,1)} %all-gather.17.cloned.1.call-done), kind=kOutput, calls=%fused_computation.75 | convolution fusion | flops 43514855424 | bytes 84443136 | tf_op jit(solution)/shard_map/btd,dhc->bthc/dot_general | solution.py:37
  646.4 31.6 %fusion.43 = bf16[16,1024,3,256]{1,3,2,0:T(8,128)(2,1)} fusion(bf16[16,1024,3,576]{1,3,2,0:T(8,128)(2,1)} %convolution_convert_fusion.3), kind=kLoop, calls=%fused_computation.71 | loop fusion | flops 100663296 | bytes 75497472 | tf_op jit(solution)/shard_map/convert_element_type | solution.py:42
  678.0 18.3 convolution_convert_fusion.7
  696.3 81.9 %fusion.160 = (f32[16,3,1024]{2,1,0:T(4,128)S(1)}, f32[16,3,1024,1024]{2,3,1,0:T(8,128)}) fusion(pred[16,1024,1024]{1,2,0:T(8,128)(4,1)} %get-tuple-element.23, bf16[16,1024,3,576]{1,3,2,0:T(8,128)(2,1)} %convolution_convert_fusion.3, bf16[16,1024,128]{1,2,0:T(8,128)(2,1)} %convolution_convert_fusion.7), kind=kOutput, calls=%fused_computation.208 | convolution fusion | flops 6643778560 | bytes 226689024 | tf_op jit(solution)/shard_map/sub | solution.py:27
  778.2 64.0 %convert_bitcast_fusion.5 = bf16[16,1024,3,64]{1,3,2,0:T(8,128)(2,1)} fusion(f32[16,3,1024,1024]{2,3,1,0:T(8,128)} %get-tuple-element.34, f32[16,3,1024]{2,1,0:T(4,128)S(1)} %get-tuple-element.33, bf16[16,1024,128]{1,2,0:T(8,128)(2,1)} %convolution_convert_fusion.7), kind=kOutput, calls=%fused_computation.148 | convolution fusion | flops 6546259968 | bytes 209911808 | tf_op jit(solution)/shard_map/bhqk,bkc->bqhc/dot_general | solution.py:28
  842.2 33.3 %bitcast_convert_fusion.3 = bf16[16,1024,768]{2,1,0:T(8,128)(2,1)} fusion(bf16[3,320,768,1]{2,1,0,3:T(8,128)(2,1)S(1)} %bitcast.262, bf16[16,1024,3,256]{1,3,2,0:T(8,128)(2,1)} %fusion.43, bf16[16,1024,3,64]{1,3,2,0:T(8,128)(2,1)} %convert_bitcast_fusion.5), kind=kOutput, calls=%fused_computation.63 | convolution fusion | flops 24234688512 | bytes 58097664 | tf_op jit(solution)/shard_map/bthc,hcd->btd/dot_general | solution.py:44
  875.5 21.0 copy.10
  924.6 253.0 %all-to-all-done = bf16[16,4,256,768]{3,2,0,1:T(8,128)(2,1)} async-done(((bf16[16,4,256,768]{3,2,0,1:T(8,128)(2,1)}), bf16[16,4,256,768]{3,2,0,1:T(8,128)(2,1)}, u32[]{:S(2)}, u32[]{:S(2)}) %all-to-all-start) | async-done | bytes 25165856 | tf_op jit(solution)/shard_map/all_to_all | solution.py:45
  1222.1 146.3 %all-gather.23.cloned.1.call-done = bf16[16,1024,768]{2,1,0:T(8,128)(2,1)} async-done(((bf16[16,256,768]{2,1,0:T(8,128)(2,1)}), bf16[16,1024,768]{2,1,0:T(8,128)(2,1)}) %all-gather.23.cloned.1.call-update) | async-done | bytes 25165840 | tf_op jit(solution)/shard_map/all_gather | solution.py:36
  1368.5 52.0 %convolution_convert_fusion = bf16[16,1024,3,576]{1,3,2,0:T(8,128)(2,1)} fusion(bf16[768,3,576,1]{0,2,1,3:T(8,128)(2,1)} %bitcast.259, bf16[16,1024,768]{2,1,0:T(8,128)(2,1)} %all-gather.23.cloned.1.call-done), kind=kOutput, calls=%fused_computation.72 | convolution fusion | flops 43514855424 | bytes 84443136 | tf_op jit(solution)/shard_map/btd,dhc->bthc/dot_general | solution.py:37
  1420.4 18.2 convolution_convert_fusion.4
  1438.7 31.5 %fusion.40 = bf16[16,1024,3,256]{1,3,2,0:T(8,128)(2,1)} fusion(bf16[16,1024,3,576]{1,3,2,0:T(8,128)(2,1)} %convolution_convert_fusion), kind=kLoop, calls=%fused_computation.68 | loop fusion | flops 100663296 | bytes 75497472 | tf_op jit(solution)/shard_map/convert_element_type | solution.py:42
  1470.2 82.0 %fusion.175 = (f32[16,3,1024]{2,1,0:T(4,128)S(1)}, f32[16,3,1024,1024]{2,3,1,0:T(8,128)}) fusion(pred[16,1024,1024]{1,2,0:T(8,128)(4,1)} %get-tuple-element.24, bf16[16,1024,3,576]{1,3,2,0:T(8,128)(2,1)} %convolution_convert_fusion, bf16[16,1024,128]{1,2,0:T(8,128)(2,1)} %convolution_convert_fusion.4), kind=kOutput, calls=%fused_computation.211 | convolution fusion | flops 6643778560 | bytes 226689024 | tf_op jit(solution)/shard_map/sub | solution.py:27
  1552.2 63.9 %convert_bitcast_fusion.2 = bf16[16,1024,3,64]{1,3,2,0:T(8,128)(2,1)} fusion(f32[16,3,1024,1024]{2,3,1,0:T(8,128)} %get-tuple-element.40, f32[16,3,1024]{2,1,0:T(4,128)S(1)} %get-tuple-element.39, bf16[16,1024,128]{1,2,0:T(8,128)(2,1)} %convolution_convert_fusion.4), kind=kOutput, calls=%fused_computation.145 | convolution fusion | flops 6546259968 | bytes 209911808 | tf_op jit(solution)/shard_map/bhqk,bkc->bqhc/dot_general | solution.py:28
  1616.1 34.0 %bitcast_convert_fusion = bf16[16,1024,768]{2,1,0:T(8,128)(2,1)} fusion(bf16[3,320,768,1]{2,1,0,3:T(8,128)(2,1)} %bitcast.263, bf16[16,1024,3,256]{1,3,2,0:T(8,128)(2,1)} %fusion.40, bf16[16,1024,3,64]{1,3,2,0:T(8,128)(2,1)} %convert_bitcast_fusion.2), kind=kOutput, calls=%fused_computation.60 | convolution fusion | flops 24234688512 | bytes 58097664 | tf_op jit(solution)/shard_map/bthc,hcd->btd/dot_general | solution.py:44
  1650.1 21.0 copy.14
  1680.0 129.8 %convolution_convert_fusion.2 = bf16[16,1024,3,576]{1,3,2,0:T(8,128)(2,1)} fusion(bf16[768,3,576,1]{0,2,1,3:T(8,128)(2,1)S(1)} %bitcast.260, bf16[16,1024,768]{2,1,0:T(8,128)(2,1)} %all-gather.19.cloned.1.call-done), kind=kOutput, calls=%fused_computation.74 | convolution fusion | flops 43514855424 | bytes 84443136 | tf_op jit(solution)/shard_map/btd,dhc->bthc/dot_general | solution.py:37
  1809.7 31.6 %fusion.42 = bf16[16,1024,3,256]{1,3,2,0:T(8,128)(2,1)} fusion(bf16[16,1024,3,576]{1,3,2,0:T(8,128)(2,1)} %convolution_convert_fusion.2), kind=kLoop, calls=%fused_computation.70 | loop fusion | flops 100663296 | bytes 75497472 | tf_op jit(solution)/shard_map/convert_element_type | solution.py:42
  1841.3 18.3 convolution_convert_fusion.6
  1859.6 81.7 %fusion.170 = (f32[16,3,1024]{2,1,0:T(4,128)S(1)}, f32[16,3,1024,1024]{2,3,1,0:T(8,128)}) fusion(pred[16,1024,1024]{1,2,0:T(8,128)(4,1)} %get-tuple-element.23, bf16[16,1024,3,576]{1,3,2,0:T(8,128)(2,1)} %convolution_convert_fusion.2, bf16[16,1024,128]{1,2,0:T(8,128)(2,1)} %convolution_convert_fusion.6), kind=kOutput, calls=%fused_computation.210 | convolution fusion | flops 6643778560 | bytes 226689024 | tf_op jit(solution)/shard_map/sub | solution.py:27
  1941.3 64.0 %convert_bitcast_fusion.4 = bf16[16,1024,3,64]{1,3,2,0:T(8,128)(2,1)} fusion(f32[16,3,1024,1024]{2,3,1,0:T(8,128)} %get-tuple-element.38, f32[16,3,1024]{2,1,0:T(4,128)S(1)} %get-tuple-element.37, bf16[16,1024,128]{1,2,0:T(8,128)(2,1)} %convolution_convert_fusion.6), kind=kOutput, calls=%fused_computation.147 | convolution fusion | flops 6546259968 | bytes 209911808 | tf_op jit(solution)/shard_map/bhqk,bkc->bqhc/dot_general | solution.py:28
  2005.3 33.4 %bitcast_convert_fusion.2 = bf16[16,1024,768]{2,1,0:T(8,128)(2,1)} fusion(bf16[3,320,768,1]{2,1,0,3:T(8,128)(2,1)S(1)} %bitcast.264, bf16[16,1024,3,256]{1,3,2,0:T(8,128)(2,1)} %fusion.42, bf16[16,1024,3,64]{1,3,2,0:T(8,128)(2,1)} %convert_bitcast_fusion.4), kind=kOutput, calls=%fused_computation.62 | convolution fusion | flops 24234688512 | bytes 58097664 | tf_op jit(solution)/shard_map/bthc,hcd->btd/dot_general | solution.py:44
  2038.7 21.0 copy.12
  2083.2 258.1 %all-to-all-done.1 = bf16[16,4,256,768]{3,2,0,1:T(8,128)(2,1)} async-done(((bf16[16,4,256,768]{3,2,0,1:T(8,128)(2,1)}), bf16[16,4,256,768]{3,2,0,1:T(8,128)(2,1)}, u32[]{:S(2)}, u32[]{:S(2)}) %all-to-all-start.1) | async-done | bytes 25165856 | tf_op jit(solution)/shard_map/all_to_all | solution.py:45
  2355.8 26.7 %fusion.109 = (bf16[2,16,256,768]{3,2,1,0:T(8,128)(2,1)}, bf16[2,16,256,768]{3,2,1,0:T(8,128)(2,1)}) fusion(f32[16,256,768]{2,1,0:T(8,128)} %convert_reduce_fusion.2, f32[16,256,768]{2,1,0:T(8,128)} %convert_reduce_fusion.3, bf16[2,16,256,768]{3,2,1,0:T(8,128)(2,1)} %param.6, ...), kind=kLoop, output_to_operand_aliasing={{0}: (5, {}), {1}: (5, {})}, calls=%fused_computation.144 | loop fusion | flops 37748736 | bytes 75497472 | tf_op jit(solution)/shard_map/convert_element_type | solution.py:47
  (94 shorter events, 203.5 us)
Async XLA Ops:
  6.5 10.8 copy-start.8
  6.5 57.5 %all-gather.25.cloned.1.call-start = ((), (), s32[]{:S(2)}) async-start(), calls=%async_computation.8 | async-start | bytes 3981312 | tf_op jit(solution)/shard_map/all_gather | solution.py:59
  10.1 195.9 %all-gather.21.cloned.1.call-start = ((), (), s32[]{:S(2)}) async-start(), calls=%async_computation.6 | async-start | bytes 31457280 | tf_op jit(solution)/shard_map/all_gather | solution.py:36
  10.1 13.7 copy-start
  28.2 7.0 copy-start.5
  28.2 9.1 copy-start.7
  28.2 18.4 copy-start.10
  35.1 417.9 %all-gather.27.cloned.1.call-start = ((), (), s32[]{:S(2)}) async-start(), calls=%async_computation.9 | async-start | bytes 2211840 | tf_op jit(solution)/shard_map/all_gather | solution.py:61
  36.4 480.2 %all-gather.17.cloned.1.call-start = ((), (), s32[]{:S(2)}) async-start(), calls=%async_computation.4 | async-start | bytes 31457280 | tf_op jit(solution)/shard_map/all_gather | solution.py:36
  46.6 211.1 %copy-start.1 = (bf16[1,768,128]{1,2,0:T(8,128)(2,1)}, bf16[1,768,128]{1,2,0:T(8,128)(2,1)S(1)}, u32[]{:S(2)}) copy-start(bf16[1,768,128]{1,2,0:T(8,128)(2,1)S(1)} %all-gather.1) | copy-start | bytes 589828
  507.8 8.8 copy-start.11
  507.8 388.7 %all-to-all-start.2 = ((bf16[16,4,256,768]{3,2,0,1:T(8,128)(2,1)}), bf16[16,4,256,768]{3,2,0,1:T(8,128)(2,1)}, u32[]{:S(2)}, u32[]{:S(2)}) async-start(bf16[16,4,256,768]{3,2,0,1:T(8,128)(2,1)} %copy.13), calls=%async_computation.2 | async-start | bytes 50331648 | tf_op jit(solution)/shard_map/all_to_all | solution.py:45
  646.4 31.6 %copy-start.2 = (bf16[1,768,128]{1,2,0:T(8,128)(2,1)S(1)}, bf16[1,768,128]{1,2,0:T(8,128)(2,1)}, u32[]{:S(2)}) copy-start(bf16[1,768,128]{1,2,0:T(8,128)(2,1)} %copy-done.1) | copy-start | bytes 589828
  778.2 64.0 %copy-start.13 = (bf16[1,960,768]{2,1,0:T(8,128)(2,1)S(1)}, bf16[1,960,768]{2,1,0:T(8,128)(2,1)}, u32[]{:S(2)}) copy-start(bf16[1,960,768]{2,1,0:T(8,128)(2,1)} %all-gather.27.cloned.1.call-done) | copy-start | bytes 4423684
  896.5 9.1 copy-start.9
  896.5 281.1 %all-to-all-start = ((bf16[16,4,256,768]{3,2,0,1:T(8,128)(2,1)}), bf16[16,4,256,768]{3,2,0,1:T(8,128)(2,1)}, u32[]{:S(2)}, u32[]{:S(2)}) async-start(bf16[16,4,256,768]{3,2,0,1:T(8,128)(2,1)} %copy.10), calls=%async_computation | async-start | bytes 50331648 | tf_op jit(solution)/shard_map/all_to_all | solution.py:45
  905.0 317.1 %all-gather.29.cloned.1.call-start = ((), (), s32[]{:S(2)}) async-start(), calls=%async_computation.10 | async-start | bytes 3981312 | tf_op jit(solution)/shard_map/all_gather | solution.py:59
  905.6 462.9 %all-gather.23.cloned.1.call-start = ((), (), s32[]{:S(2)}) async-start(), calls=%async_computation.7 | async-start | bytes 31457280 | tf_op jit(solution)/shard_map/all_gather | solution.py:36
  1209.4 7.3 copy-start.6
  1215.8 400.2 %all-gather.31.cloned.1.call-start = ((), (), s32[]{:S(2)}) async-start(), calls=%async_computation.11 | async-start | bytes 2211840 | tf_op jit(solution)/shard_map/all_gather | solution.py:61
  1216.6 463.3 %all-gather.19.cloned.1.call-start = ((), (), s32[]{:S(2)}) async-start(), calls=%async_computation.5 | async-start | bytes 31457280 | tf_op jit(solution)/shard_map/all_gather | solution.py:36
  1222.1 198.4 %copy-start.3 = (bf16[1,768,128]{1,2,0:T(8,128)(2,1)}, bf16[1,768,128]{1,2,0:T(8,128)(2,1)S(1)}, u32[]{:S(2)}) copy-start(bf16[1,768,128]{1,2,0:T(8,128)(2,1)S(1)} %all-gather.5) | copy-start | bytes 589828
  1671.1 8.8 copy-start.12
  1671.1 388.6 %all-to-all-start.3 = ((bf16[16,4,256,768]{3,2,0,1:T(8,128)(2,1)}), bf16[16,4,256,768]{3,2,0,1:T(8,128)(2,1)}, u32[]{:S(2)}, u32[]{:S(2)}) async-start(bf16[16,4,256,768]{3,2,0,1:T(8,128)(2,1)} %copy.14), calls=%async_computation.3 | async-start | bytes 50331648 | tf_op jit(solution)/shard_map/all_to_all | solution.py:45
  1809.7 31.6 %copy-start.4 = (bf16[1,768,128]{1,2,0:T(8,128)(2,1)S(1)}, bf16[1,768,128]{1,2,0:T(8,128)(2,1)}, u32[]{:S(2)}) copy-start(bf16[1,768,128]{1,2,0:T(8,128)(2,1)} %copy-done.3) | copy-start | bytes 589828
  1941.3 64.0 %copy-start.14 = (bf16[1,960,768]{2,1,0:T(8,128)(2,1)S(1)}, bf16[1,960,768]{2,1,0:T(8,128)(2,1)}, u32[]{:S(2)}) copy-start(bf16[1,960,768]{2,1,0:T(8,128)(2,1)} %all-gather.31.cloned.1.call-done) | copy-start | bytes 4423684
  2059.8 281.6 %all-to-all-start.1 = ((bf16[16,4,256,768]{3,2,0,1:T(8,128)(2,1)}), bf16[16,4,256,768]{3,2,0,1:T(8,128)(2,1)}, u32[]{:S(2)}, u32[]{:S(2)}) async-start(bf16[16,4,256,768]{3,2,0,1:T(8,128)(2,1)} %copy.12), calls=%async_computation.1 | async-start | bytes 50331648 | tf_op jit(solution)/shard_map/all_to_all | solution.py:45
Sparse Core Ops, SparseCore 0:
  10.2 41.6 all-gather.24
  53.5 152.4 all-gather.20
  207.5 22.9 all-gather.26
  231.9 152.4 all-gather.16
  907.0 37.9 all-gather.28
  1216.0 152.4 all-gather.22
  1370.0 22.9 all-gather.30
  1394.6 152.4 all-gather.18
where the time goes:
time: 2390 us
  matrix products  1150 us (48%)
  waiting for transfers between devices  801 us (34%)
  other arithmetic  270 us (11%)
  local copies, waits for them, and re-layouts  90.5 us (4%)
  starting transfers between devices  35.4 us (1%)
  blocking collectives  24 us (1%)
    all_to_all x4, waiting for transfers between devices, layer_block(): lax.all_to_all(group_sum.reshape(n_seqs, n_model, t_loc, d_model), 'model...  511 us
    dot_general x4, matrix products, layer_block(): jnp.einsum('btd,dhc->bthc', h_all, w_in3, preferred_element_type=jnp.floa...  363 us
    sub x4, matrix products, attention(): attn_probs = jax.nn.softmax(scores, axis=-1).astype(jnp.bfloat16)  327 us
    all_gather x4, waiting for transfers between devices, layer_block(): h_all = lax.all_gather(h_loc, 'model', axis=1, tiled=True)  288 us
    dot_general x4, matrix products, attention(): jnp.einsum('bhqk,bkc->bqhc', attn_probs, v_all, preferred_element_type=jn...  256 us
    dot_general x4, matrix products, layer_block(): jnp.einsum('bthc,hcd->btd', joined, w_out3, preferred_element_type=jnp.fl...  135 us
    convert_element_type x4, other arithmetic, layer_block(): (jax.nn.silu(gate_act.astype(jnp.float32)) * up_act.astype(jnp.float32))....  126 us
    reshape x4, local copies, waits for them, and re-layouts, layer_block(): group_sum.reshape(n_seqs, n_model, t_loc, d_model)  84.1 us
  transfers between devices with their start and end apart: 12, of which 4 were waited for; matrix products, arithmetic and copies ran while one was open for 62% of the time, Pallas kernels for 0%

commit v1 on v0

v1 whole, which is shorter than its diff:
```python
import functools
import jax
import jax.numpy as jnp
from jax import lax
from jax.experimental import pallas as pl
from jax.experimental.pallas import tpu as pltpu
from jax.sharding import PartitionSpec as P

NORM_EPS = 1e-6
NEG_BIG = -1e30
F32 = jnp.float32
BF16 = jnp.bfloat16


def norm_rows(x_act, gain_row):
    x_f32 = x_act.astype(F32)
    centered = x_f32 - jnp.mean(x_f32, axis=-1, keepdims=True)
    variance = jnp.mean(centered * centered, axis=-1, keepdims=True)
    return (centered * lax.rsqrt(variance + NORM_EPS) * gain_row.astype(F32)).astype(BF16)


def kv_kernel(x_ref, gain_ref, w_kv_ref, kv_ref):
    n_seqs, t_loc, d_model = x_ref.shape
    h = norm_rows(x_ref[...].reshape(n_seqs * t_loc, d_model), gain_ref[...])
    kv = jnp.dot(h, w_kv_ref[...], preferred_element_type=F32).astype(BF16)
    kv_ref[...] = kv.reshape(kv_ref.shape)


def project_kv(x, gain, w_kv, micro, block=4):
    _, n_seqs, t_loc, d_model = x.shape
    width = w_kv.shape[1]
    return pl.pallas_call(
        kv_kernel,
        grid=(n_seqs // block,),
        in_specs=[
            pl.BlockSpec((None, block, t_loc, d_model), lambda b: (micro, b, 0, 0)),
            pl.BlockSpec((1, d_model), lambda b: (0, 0)),
            pl.BlockSpec((d_model, width), lambda b: (0, 0)),
        ],
        out_specs=pl.BlockSpec((block, t_loc, width), lambda b: (b, 0, 0)),
        out_shape=jax.ShapeDtypeStruct((n_seqs, t_loc, width), BF16),
        name="kv_proj",
        cost_estimate=pl.CostEstimate(
            flops=2 * n_seqs * t_loc * d_model * width, bytes_accessed=2 * n_seqs * t_loc * (d_model + width), transcendentals=0
        ),
    )(x, gain, w_kv)


def layer_kernel(n_groups, head_dim, has_next, has_prev, *refs):
    refs = list(refs)
    pos_ref, len_ref = refs[:2]
    x_ref, kv_ref, gain_ref, w_in_hbm, w_out_hbm = refs[2:7]
    refs = refs[7:]
    if has_next:
        gain_next_ref, w_kv_next_ref = refs[:2]
        refs = refs[2:]
    if has_prev:
        refs = refs[1:]
    y_ref = refs[0]
    refs = refs[1:]
    if has_next:
        kv_next_ref = refs[0]
        refs = refs[1:]
    w_in_ref, w_out_ref, h_ref, vt_ref, acc_ref, in_sem, out_sem = refs

    t_loc, d_model = x_ref.shape
    n_chunks = kv_ref.shape[0]
    rows_out = w_out_ref.shape[1]
    half = w_out_hbm.shape[3]
    n_parts = w_out_hbm.shape[1]
    in_loc = w_in_ref.shape[2]
    ff_loc = in_loc - rows_out
    q_loc = rows_out - ff_loc
    heads = q_loc // head_dim
    seq = pl.program_id(0)

    def in_copy(group):
        return pltpu.make_async_copy(w_in_hbm.at[group], w_in_ref.at[group], in_sem.at[group])

    def out_copy(group, part):
        return pltpu.make_async_copy(
            w_out_hbm.at[group, part], w_out_ref.at[group, :, pl.ds(part * half, half)], out_sem.at[group, part]
        )

    @pl.when(seq == 0)
    def _():
        for group in range(n_groups):
            in_copy(group).start()
            for part in range(n_parts):
                out_copy(group, part).start()

    pos = pos_ref[0]
    seq_len = len_ref[seq]
    n_live = jnp.minimum(pos + 1, (seq_len + t_loc - 1) // t_loc)

    h_ref[...] = norm_rows(x_ref[...], gain_ref[...])
    vt_ref[...] = kv_ref[...].reshape(n_chunks * t_loc, 2 * head_dim).T[head_dim:]
    acc_ref[...] = jnp.zeros_like(acc_ref)

    def run(n_keys):
        chunk = n_keys - 1
        lane = lax.broadcasted_iota(jnp.int32, (1, t_loc), 1)
        limit = jnp.minimum(lane + (pos - chunk) * t_loc, seq_len - chunk * t_loc - 1)
        key = lax.broadcasted_iota(jnp.int32, (t_loc, t_loc), 0)
        keys = kv_ref[:n_keys].reshape(n_keys * t_loc, 2 * head_dim)[:, :head_dim]

        def group_step(group, carry):
            @pl.when(seq == 0)
            def _():
                in_copy(group).wait()
                for part in range(n_parts):
                    out_copy(group, part).wait()

            h = h_ref[...]
            q = jnp.dot(h, w_in_ref[group, :, 2 * ff_loc :], preferred_element_type=F32).astype(BF16)
            q_t = (q * BF16(head_dim**-0.5)).T
            joined = []
            step = 256
            for col in range(0, ff_loc, step):
                gate = jnp.dot(h, w_in_ref[group, :, col : col + step], preferred_element_type=F32).astype(BF16).astype(F32)
                up = jnp.dot(h, w_in_ref[group, :, ff_loc + col : ff_loc + col + step], preferred_element_type=F32).astype(BF16).astype(F32)
                joined.append((jax.nn.silu(gate) * up).astype(BF16))
            outs = []
            for head in range(heads):
                scores = jnp.dot(keys, q_t[head * head_dim : (head + 1) * head_dim], preferred_element_type=F32)
                last = jnp.where(key <= limit, scores[chunk * t_loc :], NEG_BIG)
                top = jnp.max(last, axis=0, keepdims=True)
                if chunk:
                    top = jnp.maximum(top, jnp.max(scores[: chunk * t_loc], axis=0, keepdims=True))
                    scores = jnp.concatenate([scores[: chunk * t_loc], last], axis=0)
                else:
                    scores = last
                weights = jnp.exp(scores - top)
                total = jnp.sum(weights, axis=0, keepdims=True)
                out_t = jnp.dot(vt_ref[:, : n_keys * t_loc], weights.astype(BF16), preferred_element_type=F32)
                outs.append((out_t / total).astype(BF16))
            joined.append(jnp.concatenate(outs, axis=0).T)
            joined = jnp.concatenate(joined, axis=1)
            z = jnp.dot(joined, w_out_ref[group], preferred_element_type=F32)
            acc_ref[...] += z.astype(BF16).astype(F32)
            return carry

        lax.fori_loop(0, n_groups, group_step, 0)

    for n_keys in range(1, n_chunks + 1):
        pl.when(n_live == n_keys)(functools.partial(run, n_keys))

    y = (x_ref[...].astype(F32) + acc_ref[...]).astype(BF16)
    y_ref[...] = y
    if has_next:
        h_next = norm_rows(y, gain_next_ref[...])
        kv_next_ref[...] = jnp.dot(h_next, w_kv_next_ref[...], preferred_element_type=F32).astype(BF16)


def run_layer(pos, lengths, x, kv, gain, w_in, w_out, head_dim, micro, next_params=None, prev=None, whole=None):
    if x.ndim == 4:
        x_spec = pl.BlockSpec((None, None) + x.shape[2:], lambda b, *_: (micro, b, 0, 0))
    else:
        x_spec = pl.BlockSpec((None,) + x.shape[1:], lambda b, *_: (b, 0, 0))
    n_seqs, t_loc, d_model = x.shape[-3:]
    n_groups, _, in_loc = w_in.shape
    _, n_parts, rows_out, _ = w_out.shape
    n_chunks = kv.shape[0]
    width = kv.shape[3]
    anywhere = pl.BlockSpec(memory_space=pl.ANY)
    in_specs = [
        x_spec,
        pl.BlockSpec((n_chunks, None, t_loc, width), lambda b, *_: (0, b, 0, 0)),
        pl.BlockSpec((1, d_model), lambda b, *_: (0, 0)),
        anywhere,
        anywhere,
    ]
    args = [x, kv, gain, w_in, w_out]
    if next_params is not None:
        in_specs += [pl.BlockSpec((1, d_model), lambda b, *_: (0, 0)), pl.BlockSpec((d_model, width), lambda b, *_: (0, 0))]
        args += list(next_params)
    aliases = {}
    if prev is not None:
        in_specs.append(anywhere)
        aliases = {2 + len(args): 0}
        args.append(prev)
    if whole is None:
        out_shape = [jax.ShapeDtypeStruct((n_seqs, t_loc, d_model), BF16)]
        out_specs = [pl.BlockSpec((None, t_loc, d_model), lambda b, *_: (b, 0, 0))]
    else:
        out_shape = [jax.ShapeDtypeStruct((whole, n_seqs, t_loc, d_model), BF16)]
        out_specs = [pl.BlockSpec((None, None, t_loc, d_model), lambda b, *_: (micro, b, 0, 0))]
    if next_params is not None:
        out_shape.append(jax.ShapeDtypeStruct((n_seqs, t_loc, width), BF16))
        out_specs.append(pl.BlockSpec((None, t_loc, width), lambda b, *_: (b, 0, 0)))
    rows = n_seqs * t_loc
    flops = 2 * rows * n_groups * d_model * (in_loc + rows_out) + 8 * rows * n_groups * n_chunks * t_loc * (rows_out * 2 - in_loc + rows_out)
    return pl.pallas_call(
        functools.partial(layer_kernel, n_groups, head_dim, next_params is not None, prev is not None),
        grid_spec=pltpu.PrefetchScalarGridSpec(
            num_scalar_prefetch=2,
            grid=(n_seqs,),
            in_specs=in_specs,
            out_specs=out_specs,
            scratch_shapes=[
                pltpu.VMEM((n_groups, d_model, in_loc), BF16),
                pltpu.VMEM((n_groups, rows_out, d_model), BF16),
                pltpu.VMEM((t_loc, d_model), BF16),
                pltpu.VMEM((head_dim, n_chunks * t_loc), BF16),
                pltpu.VMEM((t_loc, d_model), F32),
                pltpu.SemaphoreType.DMA((n_groups,)),
                pltpu.SemaphoreType.DMA((n_groups, n_parts)),
            ],
        ),
        out_shape=out_shape,
        input_output_aliases=aliases,
        name="layer",
        compiler_params=pltpu.CompilerParams(dimension_semantics=("arbitrary",), vmem_limit_bytes=60 * 2**20),
        cost_estimate=pl.CostEstimate(flops=flops, bytes_accessed=4 * rows * d_model + 2 * n_groups * d_model * (in_loc + rows_out), transcendentals=0),
    )(pos, lengths, *args)


def solution(mesh):
    n_model = mesh.shape["model"]
    act_spec = P(None, ("part", "data"), "model", None)

    def local_fn(x, lengths, gain_blk, w_in_blk, w_kv_blk, w_out_blk):
        n_micro = x.shape[0]
        n_layers, d_half, in_loc = w_in_blk.shape
        out_loc = w_out_blk.shape[1]
        head_dim = w_kv_blk.shape[2] // 2
        ff_loc = in_loc - out_loc
        heads = (out_loc - ff_loc) // head_dim
        ff_head = ff_loc // heads
        pos = lax.axis_index("model").astype(jnp.int32).reshape(1)

        gain = lax.all_gather(gain_blk, "data", axis=1, tiled=True)
        w_kv = lax.all_gather(w_kv_blk, "data", axis=1, tiled=True)

        cols = w_in_blk.reshape(n_layers, d_half, heads, in_loc // heads)
        w_in_sorted = jnp.concatenate(
            [
                cols[..., head_dim : head_dim + ff_head].reshape(n_layers, d_half, ff_loc),
                cols[..., head_dim + ff_head :].reshape(n_layers, d_half, ff_loc),
                cols[..., :head_dim].reshape(n_layers, d_half, heads * head_dim),
            ],
            axis=-1,
        )
        rows = w_out_blk.reshape(n_layers, heads, out_loc // heads, d_half)
        w_out_sorted = jnp.concatenate(
            [rows[:, :, head_dim:].reshape(n_layers, ff_loc, d_half), rows[:, :, :head_dim].reshape(n_layers, heads * head_dim, d_half)],
            axis=1,
        )

        def weights(layer):
            w_in = lax.all_gather(w_in_sorted[layer], ("model", "data"), axis=0, tiled=False)
            w_out = lax.all_gather(w_out_sorted[layer], ("model", "data"), axis=0, tiled=False)
            return w_in.reshape(n_model, -1, in_loc), w_out.reshape(n_model, -1, out_loc, d_half)

        def gains(layer):
            return gain[layer].reshape(1, -1)

        kv = [
            lax.all_gather(project_kv(x, gains(0), w_kv[0], micro), "model", axis=0, tiled=False) for micro in range(n_micro)
        ]
        hidden = [x] * n_micro
        result = None
        for layer in range(n_layers):
            w_in, w_out = weights(layer)
            last = layer == n_layers - 1
            kv_next = []
            for micro in range(n_micro):
                outs = run_layer(
                    pos, lengths[micro], hidden[micro], kv[micro], gains(layer), w_in, w_out, head_dim, micro,
                    next_params=None if last else (gains(layer + 1), w_kv[layer + 1]),
                    prev=result if last else None,
                    whole=n_micro if last else None,
                )
                if last:
                    result = outs[0]
                else:
                    hidden[micro] = outs[0]
                    kv_next.append(lax.all_gather(outs[1], "model", axis=0, tiled=False))
            kv = kv_next
        return result

    return jax.shard_map(
        local_fn,
        mesh=mesh,
        in_specs=(act_spec, P(None, ("part", "data")), P(None, "data"), P(None, "data", "model"), P(None, "data", None), P(None, "model", "data")),
        out_specs=act_spec,
        check_vma=False,
    )
```

time: 2390 us -> 961 us (0.40)
  the two profiles are of different devices: /device:TPU:0 before, /device:TPU:3 now
where the time goes in v1:
time: 961 us; the launch traced here: 949 us
  Pallas kernels  797 us (83%)
  waiting for transfers between devices  92.8 us (10%)
  local copies, waits for them, and re-layouts  34.5 us (4%)
  between operations  13.9 us (1%)
    pallas_call x4, Pallas kernels, run_layer(): pl.pallas_call(functools.partial(layer_kernel, n_groups, head_dim, next_p...  782 us
    all_gather x2, waiting for transfers between devices, weights(): lax.all_gather(w_out_sorted[layer], ('model', 'data'), axis=0, tiled=False)  40.9 us
    all_gather x2, waiting for transfers between devices, weights(): lax.all_gather(w_in_sorted[layer], ('model', 'data'), axis=0, tiled=False)  32.7 us
    all_gather x2, local copies, waits for them, and re-layouts, weights(): lax.all_gather(w_in_sorted[layer], ('model', 'data'), axis=0, tiled=False)  27.8 us
  transfers between devices with their start and end apart: 8, of which 3 were waited for; matrix products, arithmetic and copies ran while one was open for 3% of the time, Pallas kernels for 64%

profile of v1, /device:TPU:3, one launch (start us, length us, event | category | flops | bytes accessed | tf_op | source)
XLA Modules:
  0.0 949.1 jit_solution(17543880155692024244)
XLA Ops:
  6.5 1.0 slice.74
  7.5 1.9 fusion.2
  9.4 0.3 pad_maximum_fusion
  9.7 1.8 fusion.1
  11.5 0.0 all-gather.25.cloned.1.call-start
  11.6 3.2 all_gather.42
  14.8 5.2 all_gather.43
  19.9 0.6 fusion.3
  20.5 0.8 slice_bitcast_fusion
  21.3 7.6 kv_proj.3
  28.9 0.0 all-gather.15.cloned.1.call-start
  29.0 0.1 slice.76
  29.1 1.3 pad_maximum_fusion.1
  30.4 0.0 all-gather.21.cloned.1.call-start
  30.5 7.5 kv_proj.2
  38.0 0.0 all-gather.17.cloned.1.call-start
  38.0 0.5 all-gather.17.cloned.1.call-update
  38.6 0.0 all-gather.19.cloned.1.call-start
  38.6 0.5 all-gather.19.cloned.1.call-update
  39.1 0.6 all-gather.27.cloned.1.call-start
  39.7 0.5 slice_bitcast_fusion.2
  40.3 32.7 %all-gather.13.cloned.1.call-done = bf16[8,384,1728]{1,2,0:T(8,128)(2,1)} async-done(((bf16[1,384,1728]{1,2,0:T(8,128)(2,1)}), bf16[8,384,1728]{1,2,0:T(8,128)(2,1)}) %all-gather.13.cloned.1.call-update) | async-done | bytes 10616848 | tf_op jit(solution)/shard_map/all_gather | solution.py:251
  73.0 13.9 %copy.13 = bf16[8,384,1728]{2,1,0:T(8,128)(2,1)} copy(bf16[8,384,1728]{1,2,0:T(8,128)(2,1)} %all-gather.13.cloned.1.call-done) | data formatting | bytes 21233664 | tf_op jit(solution)/shard_map/all_gather | solution.py:251
  86.9 18.0 %all-gather.25.cloned.1.call-done = bf16[64,256,128]{2,1,0:T(8,128)(2,1)} async-done(((bf16[16,256,128]{2,1,0:T(8,128)(2,1)}), bf16[64,256,128]{2,1,0:T(8,128)(2,1)}) %all-gather.25.cloned.1.call-update) | async-done | bytes 4194320 | tf_op jit(solution)/shard_map/all_gather | solution.py:259
  104.9 40.9 %all-gather.15.cloned.1.call-done = bf16[8,960,384]{2,1,0:T(8,128)(2,1)} async-done(((bf16[1,960,384]{2,1,0:T(8,128)(2,1)}), bf16[8,960,384]{2,1,0:T(8,128)(2,1)}) %all-gather.15.cloned.1.call-update) | async-done | bytes 5898256 | tf_op jit(solution)/shard_map/all_gather | solution.py:252
  145.8 197.4 %layer.5 = (bf16[16,256,768]{2,1,0:T(8,128)(2,1)}, bf16[16,256,128]{2,1,0:T(8,128)(2,1)}) custom-call(s32[1]{0:T(128)} %bitcast.refs_0_, s32[16]{0:T(128)} %get-tuple-element.23.refs_1_, bf16[2,16,256,768]{3,2,1,0:T(8,128)(2,1)} %refs_2_.3, bf16[4,16,256,128]{3,2,1,0:T(8,128)(2,1)} %bitcast.41, bf16[1,768]{1,0:T(2,128)(2,1)} %get-tuple-element.22.gain_ref.refs_4_, ...), custom_call_target="tpu_custom_call" | custom-call | flops 222264557568 | bytes 29097984 | tf_op jit(solution)/shard_map/layer/pallas_call | solution.py:193
  343.2 0.2 all-gather.23.cloned.1.call-start
  343.5 200.6 %layer.4 = (bf16[16,256,768]{2,1,0:T(8,128)(2,1)}, bf16[16,256,128]{2,1,0:T(8,128)(2,1)}) custom-call(s32[1]{0:T(128)} %bitcast.refs_0_, s32[16]{0:T(128)} %get-tuple-element.24.refs_1_, bf16[2,16,256,768]{3,2,1,0:T(8,128)(2,1)} %refs_2_.3, bf16[4,16,256,128]{3,2,1,0:T(8,128)(2,1)} %bitcast.42, bf16[1,768]{1,0:T(2,128)(2,1)} %get-tuple-element.22.gain_ref.refs_4_, ...), custom_call_target="tpu_custom_call" | custom-call | flops 222264557568 | bytes 29097984 | tf_op jit(solution)/shard_map/layer/pallas_call | solution.py:193
  544.2 13.9 %copy.14 = bf16[8,384,1728]{2,1,0:T(8,128)(2,1)} copy(bf16[8,384,1728]{1,2,0:T(8,128)(2,1)} %all-gather.17.cloned.1.call-done) | data formatting | bytes 21233664 | tf_op jit(solution)/shard_map/all_gather | solution.py:251
  558.0 190.3 %layer.6.refs_7_ = bf16[2,16,256,768]{3,2,1,0:T(8,128)(2,1)} custom-call(s32[1]{0:T(128)} %bitcast.refs_0_, s32[16]{0:T(128)} %get-tuple-element.23.refs_1_, bf16[16,256,768]{2,1,0:T(8,128)(2,1)} %get-tuple-element.11.refs_2_, bf16[4,16,256,128]{3,2,1,0:T(8,128)(2,1)} %bitcast.43, bf16[1,768]{1,0:T(2,128)(2,1)} %get-tuple-element.21.refs_7_.refs_4_, ...), custom_call_target="tpu_custom_call" | custom-call | flops 222264557568 | bytes 29097984 | tf_op jit(solution)/shard_map/layer/pallas_call | solution.py:193
  748.4 0.0 all-gather.23.cloned.1.call-done
  748.4 193.5 %layer.7 = bf16[2,16,256,768]{3,2,1,0:T(8,128)(2,1)} custom-call(s32[1]{0:T(128)} %bitcast.refs_0_, s32[16]{0:T(128)} %get-tuple-element.24.refs_1_, bf16[16,256,768]{2,1,0:T(8,128)(2,1)} %get-tuple-element.9.refs_2_, bf16[4,16,256,128]{3,2,1,0:T(8,128)(2,1)} %bitcast.44, ...), custom_call_target="tpu_custom_call", output_to_operand_aliasing={{}: (7, {})} | custom-call | flops 222264557568 | bytes 29097984 | tf_op jit(solution)/shard_map/layer/pallas_call | solution.py:193
  (20 shorter events, 0.2 us)
Async XLA Ops:
  6.5 66.4 %all-gather.13.cloned.1.call-start = ((), (), s32[]{:S(2)}) async-start(), calls=%async_computation | async-start | bytes 11943936 | tf_op jit(solution)/shard_map/all_gather | solution.py:251
  9.7 1.9 copy-start.2
  9.7 5.1 copy-start.1
  11.5 93.4 %all-gather.25.cloned.1.call-start = ((), (), s32[]{:S(2)}) async-start(), calls=%async_computation.6 | async-start | bytes 5242880 | tf_op jit(solution)/shard_map/all_gather | solution.py:259
  21.3 7.6 copy-start
  28.9 116.9 %all-gather.15.cloned.1.call-start = ((), (), s32[]{:S(2)}) async-start(), calls=%async_computation.1 | async-start | bytes 6635520 | tf_op jit(solution)/shard_map/all_gather | solution.py:252
  30.4 313.1 %all-gather.21.cloned.1.call-start = ((), (), s32[]{:S(2)}) async-start(), calls=%async_computation.4 | async-start | bytes 5242880 | tf_op jit(solution)/shard_map/all_gather | solution.py:259
  37.9 1.8 copy-start.3
  38.0 506.2 %all-gather.17.cloned.1.call-start = ((), (), s32[]{:S(2)}) async-start(), calls=%async_computation.2 | async-start | bytes 11943936 | tf_op jit(solution)/shard_map/all_gather | solution.py:251
  38.6 519.5 %all-gather.19.cloned.1.call-start = ((), (), s32[]{:S(2)}) async-start(), calls=%async_computation.3 | async-start | bytes 6635520 | tf_op jit(solution)/shard_map/all_gather | solution.py:252
  39.1 518.9 %all-gather.27.cloned.1.call-start = ((), (), s32[]{:S(2)}) async-start(), calls=%async_computation.7 | async-start | bytes 5242880 | tf_op jit(solution)/shard_map/all_gather | solution.py:278
  343.2 405.2 %all-gather.23.cloned.1.call-start = ((), (), s32[]{:S(2)}) async-start(), calls=%async_computation.5 | async-start | bytes 5242880 | tf_op jit(solution)/shard_map/all_gather | solution.py:278
Sparse Core Ops, SparseCore 0:
  11.6 61.3 all-gather.12
  74.5 30.3 all-gather.24
  106.7 38.9 all-gather.14
  147.2 30.3 all-gather.20
  179.2 59.0 all-gather.16
  240.0 37.8 all-gather.18
  343.4 35.2 all-gather.26
  544.2 34.1 all-gather.22

commit v2 on v1

--- a/solution.py
+++ b/solution.py
@@ -49,8 +49,8 @@
 def layer_kernel(n_groups, head_dim, has_next, has_prev, *refs):
     refs = list(refs)
     pos_ref, len_ref = refs[:2]
-    x_ref, kv_ref, gain_ref, w_in_hbm, w_out_hbm = refs[2:7]
-    refs = refs[7:]
+    x_after_ref, x_before_ref, kv_ref, kv_after_ref, gain_ref, w_in_hbm, w_out_hbm = refs[2:9]
+    refs = refs[9:]
     if has_next:
         gain_next_ref, w_kv_next_ref = refs[:2]
         refs = refs[2:]
@@ -61,9 +61,9 @@
     if has_next:
         kv_next_ref = refs[0]
         refs = refs[1:]
-    w_in_ref, w_out_ref, h_ref, vt_ref, acc_ref, in_sem, out_sem = refs
-
-    t_loc, d_model = x_ref.shape
+    w_in_ref, w_out_ref, h_ref, vt_ref, joined_ref, acc_ref, s_ref, p_ref, in_sem, out_sem = refs
+
+    t_loc, d_model = x_after_ref.shape
     n_chunks = kv_ref.shape[0]
     rows_out = w_out_ref.shape[1]
     half = w_out_hbm.shape[3]
@@ -72,7 +72,10 @@
     ff_loc = in_loc - rows_out
     q_loc = rows_out - ff_loc
     heads = q_loc // head_dim
-    seq = pl.program_id(0)
+    step = pl.program_id(0)
+    n_seqs = pl.num_programs(0) - 1
+    tile = 256
+    rows_part = t_loc // 2
 
     def in_copy(group):
         return pltpu.make_async_copy(w_in_hbm.at[group], w_in_ref.at[group], in_sem.at[group])
@@ -82,95 +85,205 @@
             w_out_hbm.at[group, part], w_out_ref.at[group, :, pl.ds(part * half, half)], out_sem.at[group, part]
         )
 
-    @pl.when(seq == 0)
+    pos = pos_ref[0]
+    slot = lax.rem(step, 2)
+    other = 1 - slot
+
+    def normalize_part(dst, src_ref, part):
+        rows = pl.ds(part * rows_part, rows_part)
+        h_ref[dst, rows] = norm_rows(src_ref[rows], gain_ref[...])
+
+    def transpose_part(dst, src_ref, part):
+        span = n_chunks // 2
+        block = src_ref[pl.ds(part * span, span)].reshape(span * t_loc, 2 * head_dim)
+        vt_ref[dst, part] = block.T[head_dim:]
+
+    def epilogue_part(src, part):
+        rows = pl.ds(part * rows_part, rows_part)
+        y = (x_before_ref[rows].astype(F32) + acc_ref[src, rows]).astype(BF16)
+        y_ref[rows] = y
+        if has_next:
+            h_next = norm_rows(y, gain_next_ref[...])
+            kv_next_ref[rows] = jnp.dot(h_next, w_kv_next_ref[...], preferred_element_type=F32).astype(BF16)
+
+    def project_out(joined_slot, group, dst, fresh, col):
+        cols = slice(col, col + tile)
+        z = jnp.dot(joined_ref[joined_slot], w_out_ref[group, :, cols], preferred_element_type=F32)
+        z = z.astype(BF16).astype(F32)
+        base = acc_ref[dst, :, cols]
+        if fresh is not None:
+            base = jnp.where(fresh, 0.0, base)
+        acc_ref[dst, :, cols] = base + z
+
+    @pl.when(step == 0)
     def _():
         for group in range(n_groups):
             in_copy(group).start()
             for part in range(n_parts):
-                out_copy(group, part).start()
-
-    pos = pos_ref[0]
-    seq_len = len_ref[seq]
-    n_live = jnp.minimum(pos + 1, (seq_len + t_loc - 1) // t_loc)
-
-    h_ref[...] = norm_rows(x_ref[...], gain_ref[...])
-    vt_ref[...] = kv_ref[...].reshape(n_chunks * t_loc, 2 * head_dim).T[head_dim:]
-    acc_ref[...] = jnp.zeros_like(acc_ref)
+                out_copy(n_groups - 1 if group == 0 else group - 1, part).start()
+        for part in range(2):
+            normalize_part(slot, x_before_ref, part)
+            transpose_part(slot, kv_ref, part)
+        joined_ref[1] = jnp.zeros_like(joined_ref[1])
+        acc_ref[1] = jnp.zeros_like(acc_ref[1])
+
+    @pl.when(step == n_seqs)
+    def _():
+        for col in range(0, d_model, tile):
+            project_out(1, n_groups - 1, other, None, col)
+        for part in range(2):
+            epilogue_part(other, part)
 
     def run(n_keys):
         chunk = n_keys - 1
+        seq_len = len_ref[jnp.minimum(step, n_seqs - 1)]
         lane = lax.broadcasted_iota(jnp.int32, (1, t_loc), 1)
         limit = jnp.minimum(lane + (pos - chunk) * t_loc, seq_len - chunk * t_loc - 1)
         key = lax.broadcasted_iota(jnp.int32, (t_loc, t_loc), 0)
-        keys = kv_ref[:n_keys].reshape(n_keys * t_loc, 2 * head_dim)[:, :head_dim]
-
-        def group_step(group, carry):
-            @pl.when(seq == 0)
+
+        def trip(pair, carry):
+            first = 2 * pair
+            before = lax.rem(first + n_groups - 1, n_groups)
+
+            @pl.when(step == 0)
             def _():
-                in_copy(group).wait()
+                @pl.when(pair == 0)
+                def _():
+                    for part in range(n_parts):
+                        out_copy(n_groups - 1, part).wait()
+
+                @pl.when(pair != 0)
+                def _():
+                    for part in range(n_parts):
+                        out_copy(before, part).wait()
+
+                in_copy(first).wait()
+                in_copy(first + 1).wait()
                 for part in range(n_parts):
-                    out_copy(group, part).wait()
-
-            h = h_ref[...]
-            q = jnp.dot(h, w_in_ref[group, :, 2 * ff_loc :], preferred_element_type=F32).astype(BF16)
-            q_t = (q * BF16(head_dim**-0.5)).T
-            joined = []
-            step = 256
-            for col in range(0, ff_loc, step):
-                gate = jnp.dot(h, w_in_ref[group, :, col : col + step], preferred_element_type=F32).astype(BF16).astype(F32)
-                up = jnp.dot(h, w_in_ref[group, :, ff_loc + col : ff_loc + col + step], preferred_element_type=F32).astype(BF16).astype(F32)
-                joined.append((jax.nn.silu(gate) * up).astype(BF16))
-            outs = []
-            for head in range(heads):
-                scores = jnp.dot(keys, q_t[head * head_dim : (head + 1) * head_dim], preferred_element_type=F32)
-                last = jnp.where(key <= limit, scores[chunk * t_loc :], NEG_BIG)
-                top = jnp.max(last, axis=0, keepdims=True)
-                if chunk:
-                    top = jnp.maximum(top, jnp.max(scores[: chunk * t_loc], axis=0, keepdims=True))
-                    scores = jnp.concatenate([scores[: chunk * t_loc], last], axis=0)
+                    out_copy(first, part).wait()
+
+            h = h_ref[slot]
+            dst_before = jnp.where(pair == 0, other, slot)
+            queries = {}
+            tops = {}
+            sums = {}
+
+            def query(sub):
+                q = jnp.dot(h, w_in_ref[first + sub, :, 2 * ff_loc :], preferred_element_type=F32).astype(BF16)
+                queries[sub] = (q * BF16(head_dim**-0.5)).T
+
+            def gate_up(sub, part):
+                col = part * tile
+                gate = jnp.dot(h, w_in_ref[first + sub, :, col : col + tile], preferred_element_type=F32).astype(BF16).astype(F32)
+                up = jnp.dot(h, w_in_ref[first + sub, :, ff_loc + col : ff_loc + col + tile], preferred_element_type=F32).astype(BF16).astype(F32)
+                joined_ref[sub, :, col : col + tile] = (jax.nn.silu(gate) * up).astype(BF16)
+
+            def score(sub, head):
+                q_t = queries[sub][head * head_dim : (head + 1) * head_dim]
+                best = None
+                for c in range(n_keys):
+                    s = jnp.dot(kv_ref[c, :, :head_dim], q_t, preferred_element_type=F32)
+                    if c == chunk:
+                        s = jnp.where(key <= limit, s, NEG_BIG)
+                    s_ref[head, c * t_loc : (c + 1) * t_loc] = s
+                    m = jnp.max(s.reshape(t_loc // 8, 8, t_loc), axis=0)
+                    best = m if best is None else jnp.maximum(best, m)
+                tops[sub, head] = jnp.max(best, axis=0, keepdims=True)
+
+            def softmax(sub, head):
+                total = None
+                top = tops[sub, head]
+                width = 64
+                for r in range(0, n_keys * t_loc, width):
+                    e = jnp.exp(s_ref[head, r : r + width] - top)
+                    t = jnp.sum(e.reshape(width // 8, 8, t_loc), axis=0)
+                    total = t if total is None else total + t
+                    p_ref[head, r : r + width] = e.astype(BF16)
+                sums[sub, head] = jnp.sum(total, axis=0, keepdims=True)
+
+            outs = {}
+
+            def value(sub, head):
+                span = n_chunks // 2 * t_loc
+                out_t = None
+                for part in range(2):
+                    size = min(span, n_keys * t_loc - part * span)
+                    if size <= 0:
+                        continue
+                    o = jnp.dot(vt_ref[slot, part, :, :size], p_ref[head, part * span : part * span + size], preferred_element_type=F32)
+                    out_t = o if out_t is None else out_t + o
+                outs[sub, head] = (out_t / sums[sub, head]).astype(BF16)
+                if head == heads - 1:
+                    joined_ref[sub, :, ff_loc:] = jnp.concatenate([outs[sub, i] for i in range(heads)], axis=0).T
+
+            for sub in range(2):
+                query(sub)
+                if sub == 0:
+                    z = lambda i: project_out(1, before, dst_before, None, i * tile)
                 else:
-                    scores = last
-                weights = jnp.exp(scores - top)
-                total = jnp.sum(weights, axis=0, keepdims=True)
-                out_t = jnp.dot(vt_ref[:, : n_keys * t_loc], weights.astype(BF16), preferred_element_type=F32)
-                outs.append((out_t / total).astype(BF16))
-            joined.append(jnp.concatenate(outs, axis=0).T)
-            joined = jnp.concatenate(joined, axis=1)
-            z = jnp.dot(joined, w_out_ref[group], preferred_element_type=F32)
-            acc_ref[...] += z.astype(BF16).astype(F32)
+                    z = lambda i: project_out(0, first, slot, pair == 0, i * tile)
+                z(0)
+                score(sub, 0)
+                z(1)
+                score(sub, 1)
+                softmax(sub, 0)
+                z(2)
+                gate_up(sub, 0)
+                score(sub, 2)
+                softmax(sub, 1)
+                value(sub, 0)
+                gate_up(sub, 1)
+                softmax(sub, 2)
+                value(sub, 1)
+                gate_up(sub, 2)
+                value(sub, 2)
+                if sub == 0:
+                    normalize_part(other, x_after_ref, pair)
+                    transpose_part(other, kv_after_ref, pair)
+                else:
+                    epilogue_part(other, pair)
             return carry
 
-        lax.fori_loop(0, n_groups, group_step, 0)
-
+        lax.fori_loop(0, n_groups // 2, trip, 0)
+
+    seq_len = len_ref[jnp.minimum(step, n_seqs - 1)]
+    n_live = jnp.minimum(pos + 1, (seq_len + t_loc - 1) // t_loc)
     for n_keys in range(1, n_chunks + 1):
-        pl.when(n_live == n_keys)(functools.partial(run, n_keys))
-
-    y = (x_ref[...].astype(F32) + acc_ref[...]).astype(BF16)
-    y_ref[...] = y
-    if has_next:
-        h_next = norm_rows(y, gain_next_ref[...])
-        kv_next_ref[...] = jnp.dot(h_next, w_kv_next_ref[...], preferred_element_type=F32).astype(BF16)
+        pl.when(jnp.logical_and(n_live == n_keys, step < n_seqs))(functools.partial(run, n_keys))
 
 
 def run_layer(pos, lengths, x, kv, gain, w_in, w_out, head_dim, micro, next_params=None, prev=None, whole=None):
-    if x.ndim == 4:
-        x_spec = pl.BlockSpec((None, None) + x.shape[2:], lambda b, *_: (micro, b, 0, 0))
-    else:
-        x_spec = pl.BlockSpec((None,) + x.shape[1:], lambda b, *_: (b, 0, 0))
     n_seqs, t_loc, d_model = x.shape[-3:]
+
+    def after(b):
+        return jnp.minimum(b + 1, n_seqs - 1)
+
+    def now(b):
+        return jnp.minimum(b, n_seqs - 1)
+
+    def before(b):
+        return jnp.maximum(b - 1, 0)
+
+    def x_spec(seq):
+        if x.ndim == 4:
+            return pl.BlockSpec((None, None) + x.shape[2:], lambda b, *_: (micro, seq(b), 0, 0))
+        return pl.BlockSpec((None,) + x.shape[1:], lambda b, *_: (seq(b), 0, 0))
+
     n_groups, _, in_loc = w_in.shape
     _, n_parts, rows_out, _ = w_out.shape
     n_chunks = kv.shape[0]
     width = kv.shape[3]
     anywhere = pl.BlockSpec(memory_space=pl.ANY)
     in_specs = [
-        x_spec,
-        pl.BlockSpec((n_chunks, None, t_loc, width), lambda b, *_: (0, b, 0, 0)),
+        x_spec(after),
+        x_spec(before),
+        pl.BlockSpec((n_chunks, None, t_loc, width), lambda b, *_: (0, now(b), 0, 0)),
+        pl.BlockSpec((n_chunks, None, t_loc, width), lambda b, *_: (0, after(b), 0, 0)),
         pl.BlockSpec((1, d_model), lambda b, *_: (0, 0)),
         anywhere,
         anywhere,
     ]
-    args = [x, kv, gain, w_in, w_out]
+    args = [x, x, kv, kv, gain, w_in, w_out]
     if next_params is not None:
         in_specs += [pl.BlockSpec((1, d_model), lambda b, *_: (0, 0)), pl.BlockSpec((d_model, width), lambda b, *_: (0, 0))]
         args += list(next_params)
@@ -181,28 +294,32 @@
         args.append(prev)
     if whole is None:
         out_shape = [jax.ShapeDtypeStruct((n_seqs, t_loc, d_model), BF16)]
-        out_specs = [pl.BlockSpec((None, t_loc, d_model), lambda b, *_: (b, 0, 0))]
+        out_specs = [pl.BlockSpec((None, t_loc, d_model), lambda b, *_: (before(b), 0, 0))]
     else:
         out_shape = [jax.ShapeDtypeStruct((whole, n_seqs, t_loc, d_model), BF16)]
-        out_specs = [pl.BlockSpec((None, None, t_loc, d_model), lambda b, *_: (micro, b, 0, 0))]
+        out_specs = [pl.BlockSpec((None, None, t_loc, d_model), lambda b, *_: (micro, before(b), 0, 0))]
     if next_params is not None:
         out_shape.append(jax.ShapeDtypeStruct((n_seqs, t_loc, width), BF16))
-        out_specs.append(pl.BlockSpec((None, t_loc, width), lambda b, *_: (b, 0, 0)))
+        out_specs.append(pl.BlockSpec((None, t_loc, width), lambda b, *_: (before(b), 0, 0)))
     rows = n_seqs * t_loc
+    heads = (2 * rows_out - in_loc) // head_dim
     flops = 2 * rows * n_groups * d_model * (in_loc + rows_out) + 8 * rows * n_groups * n_chunks * t_loc * (rows_out * 2 - in_loc + rows_out)
     return pl.pallas_call(
         functools.partial(layer_kernel, n_groups, head_dim, next_params is not None, prev is not None),
         grid_spec=pltpu.PrefetchScalarGridSpec(
             num_scalar_prefetch=2,
-            grid=(n_seqs,),
+            grid=(n_seqs + 1,),
             in_specs=in_specs,
             out_specs=out_specs,
             scratch_shapes=[
                 pltpu.VMEM((n_groups, d_model, in_loc), BF16),
                 pltpu.VMEM((n_groups, rows_out, d_model), BF16),
-                pltpu.VMEM((t_loc, d_model), BF16),
-                pltpu.VMEM((head_dim, n_chunks * t_loc), BF16),
-                pltpu.VMEM((t_loc, d_model), F32),
+                pltpu.VMEM((2, t_loc, d_model), BF16),
+                pltpu.VMEM((2, 2, head_dim, n_chunks // 2 * t_loc), BF16),
+                pltpu.VMEM((2, t_loc, rows_out), BF16),
+                pltpu.VMEM((2, t_loc, d_model), F32),
+                pltpu.VMEM((heads, n_chunks * t_loc, t_loc), F32),
+                pltpu.VMEM((heads, n_chunks * t_loc, t_loc), BF16),
                 pltpu.SemaphoreType.DMA((n_groups,)),
                 pltpu.SemaphoreType.DMA((n_groups, n_parts)),
             ],

time: 961 us -> 773 us (0.80)
  the two profiles are of different devices: /device:TPU:3 before, /device:TPU:7 now
where the time goes in v2:
time: 773 us; the launch traced here: 768 us
  Pallas kernels  617 us (80%)
  waiting for transfers between devices  92.4 us (12%)
  local copies, waits for them, and re-layouts  34.5 us (4%)
  between operations  14 us (2%)
  blocking collectives  8.37 us (1%)
    pallas_call x4, Pallas kernels, run_layer(): pl.pallas_call(functools.partial(layer_kernel, n_groups, head_dim, next_p...  602 us
    all_gather x2, waiting for transfers between devices, weights(): lax.all_gather(w_out_sorted[layer], ('model', 'data'), axis=0, tiled=False)  39.7 us
    all_gather x2, waiting for transfers between devices, weights(): lax.all_gather(w_in_sorted[layer], ('model', 'data'), axis=0, tiled=False)  32.3 us
    all_gather x2, local copies, waits for them, and re-layouts, weights(): lax.all_gather(w_in_sorted[layer], ('model', 'data'), axis=0, tiled=False)  27.8 us
    all_gather x2, waiting for transfers between devices, local_fn(): lax.all_gather(project_kv(x, gains(0), w_kv[0], micro), 'model', axis=0,...  19.2 us
  transfers between devices with their start and end apart: 8, of which 3 were waited for; matrix products, arithmetic and copies ran while one was open for 4% of the time, Pallas kernels for 61%

profile of v2, /device:TPU:7, one launch (start us, length us, event | category | flops | bytes accessed | tf_op | source)
XLA Modules:
  0.0 768.0 jit_solution(10576603734286708336)
XLA Ops:
  6.5 1.0 slice.74
  7.5 1.9 fusion.2
  9.4 0.3 pad_maximum_fusion
  9.7 1.8 fusion.1
  11.5 0.0 all-gather.25.cloned.1.call-start
  11.6 3.2 all_gather.42
  14.8 5.2 all_gather.43
  19.9 0.6 fusion.3
  20.5 0.8 slice_bitcast_fusion
  21.3 7.6 kv_proj.3
  28.9 0.0 all-gather.15.cloned.1.call-start
  29.0 0.1 slice.76
  29.1 1.3 pad_maximum_fusion.1
  30.4 0.0 all-gather.21.cloned.1.call-start
  30.5 7.5 kv_proj.2
  38.0 0.0 all-gather.17.cloned.1.call-start
  38.0 0.5 all-gather.17.cloned.1.call-update
  38.6 0.0 all-gather.19.cloned.1.call-start
  38.6 0.5 all-gather.19.cloned.1.call-update
  39.1 0.0 all-gather.27.cloned.1.call-start
  39.2 0.5 slice_bitcast_fusion.2
  39.7 32.3 %all-gather.13.cloned.1.call-done = bf16[8,384,1728]{1,2,0:T(8,128)(2,1)} async-done(((bf16[1,384,1728]{1,2,0:T(8,128)(2,1)}), bf16[8,384,1728]{1,2,0:T(8,128)(2,1)}) %all-gather.13.cloned.1.call-update) | async-done | bytes 10616848 | tf_op jit(solution)/shard_map/all_gather | solution.py:368
  72.0 13.9 %copy.13 = bf16[8,384,1728]{2,1,0:T(8,128)(2,1)} copy(bf16[8,384,1728]{1,2,0:T(8,128)(2,1)} %all-gather.13.cloned.1.call-done) | data formatting | bytes 21233664 | tf_op jit(solution)/shard_map/all_gather | solution.py:368
  85.9 19.2 %all-gather.25.cloned.1.call-done = bf16[64,256,128]{2,1,0:T(8,128)(2,1)} async-done(((bf16[16,256,128]{2,1,0:T(8,128)(2,1)}), bf16[64,256,128]{2,1,0:T(8,128)(2,1)}) %all-gather.25.cloned.1.call-update) | async-done | bytes 4194320 | tf_op jit(solution)/shard_map/all_gather | solution.py:376
  105.1 39.7 %all-gather.15.cloned.1.call-done = bf16[8,960,384]{2,1,0:T(8,128)(2,1)} async-done(((bf16[1,960,384]{2,1,0:T(8,128)(2,1)}), bf16[8,960,384]{2,1,0:T(8,128)(2,1)}) %all-gather.15.cloned.1.call-update) | async-done | bytes 5898256 | tf_op jit(solution)/shard_map/all_gather | solution.py:369
  144.8 159.7 %layer.5 = (bf16[16,256,768]{2,1,0:T(8,128)(2,1)}, bf16[16,256,128]{2,1,0:T(8,128)(2,1)}) custom-call(s32[1]{0:T(128)} %bitcast.refs_0_, s32[16]{0:T(128)} %get-tuple-element.23.refs_1_, bf16[2,16,256,768]{3,2,1,0:T(8,128)(2,1)} %refs_3_.3, bf16[2,16,256,768]{3,2,1,0:T(8,128)(2,1)} %refs_3_.3, bf16[4,16,256,128]{3,2,1,0:T(8,128)(2,1)} %bitcast.41, ...), custom_call_target="tpu_custom_call" | custom-call | flops 222264557568 | bytes 29097984 | tf_op jit(solution)/shard_map/layer/pallas_call | solution.py:307
  304.5 0.0 all-gather.23.cloned.1.call-start
  304.6 150.5 %layer.4 = (bf16[16,256,768]{2,1,0:T(8,128)(2,1)}, bf16[16,256,128]{2,1,0:T(8,128)(2,1)}) custom-call(s32[1]{0:T(128)} %bitcast.refs_0_, s32[16]{0:T(128)} %get-tuple-element.24.refs_1_, bf16[2,16,256,768]{3,2,1,0:T(8,128)(2,1)} %refs_3_.3, bf16[2,16,256,768]{3,2,1,0:T(8,128)(2,1)} %refs_3_.3, bf16[4,16,256,128]{3,2,1,0:T(8,128)(2,1)} %bitcast.43, ...), custom_call_target="tpu_custom_call" | custom-call | flops 222264557568 | bytes 29097984 | tf_op jit(solution)/shard_map/layer/pallas_call | solution.py:307
  455.2 0.0 all-gather.17.cloned.1.call-done
  455.2 13.9 %copy.14 = bf16[8,384,1728]{2,1,0:T(8,128)(2,1)} copy(bf16[8,384,1728]{1,2,0:T(8,128)(2,1)} %all-gather.17.cloned.1.call-done) | data formatting | bytes 21233664 | tf_op jit(solution)/shard_map/all_gather | solution.py:368
  469.1 144.9 %layer.6.refs_9_ = bf16[2,16,256,768]{3,2,1,0:T(8,128)(2,1)} custom-call(s32[1]{0:T(128)} %bitcast.refs_0_, s32[16]{0:T(128)} %get-tuple-element.23.refs_1_, bf16[16,256,768]{2,1,0:T(8,128)(2,1)} %get-tuple-element.11.refs_2_.refs_3_, bf16[16,256,768]{2,1,0:T(8,128)(2,1)} %get-tuple-element.11.refs_2_.refs_3_, bf16[4,16,256,128]{3,2,1,0:T(8,128)(2,1)} %bitcast.45, ...), custom_call_target="tpu_custom_call" | custom-call | flops 222264557568 | bytes 29097984 | tf_op jit(solution)/shard_map/layer/pallas_call | solution.py:307
  614.0 146.8 %layer.7 = bf16[2,16,256,768]{3,2,1,0:T(8,128)(2,1)} custom-call(s32[1]{0:T(128)} %bitcast.refs_0_, s32[16]{0:T(128)} %get-tuple-element.24.refs_1_, bf16[16,256,768]{2,1,0:T(8,128)(2,1)} %get-tuple-element.9.refs_2_.refs_3_, bf16[16,256,768]{2,1,0:T(8,128)(2,1)} %get-tuple-element.9.refs_2_.refs_3_, ...), custom_call_target="tpu_custom_call", output_to_operand_aliasing={{}: (9, {})} | custom-call | flops 222264557568 | bytes 29097984 | tf_op jit(solution)/shard_map/layer/pallas_call | solution.py:307
  (20 shorter events, 0.2 us)
Async XLA Ops:
  6.5 65.5 %all-gather.13.cloned.1.call-start = ((), (), s32[]{:S(2)}) async-start(), calls=%async_computation | async-start | bytes 11943936 | tf_op jit(solution)/shard_map/all_gather | solution.py:368
  9.7 1.9 copy-start.2
  9.7 5.1 copy-start.1
  11.5 93.6 %all-gather.25.cloned.1.call-start = ((), (), s32[]{:S(2)}) async-start(), calls=%async_computation.6 | async-start | bytes 5242880 | tf_op jit(solution)/shard_map/all_gather | solution.py:376
  21.3 7.6 copy-start
  28.9 115.9 %all-gather.15.cloned.1.call-start = ((), (), s32[]{:S(2)}) async-start(), calls=%async_computation.1 | async-start | bytes 6635520 | tf_op jit(solution)/shard_map/all_gather | solution.py:369
  30.4 274.2 %all-gather.21.cloned.1.call-start = ((), (), s32[]{:S(2)}) async-start(), calls=%async_computation.4 | async-start | bytes 5242880 | tf_op jit(solution)/shard_map/all_gather | solution.py:376
  37.9 1.2 copy-start.3
  38.0 417.2 %all-gather.17.cloned.1.call-start = ((), (), s32[]{:S(2)}) async-start(), calls=%async_computation.2 | async-start | bytes 11943936 | tf_op jit(solution)/shard_map/all_gather | solution.py:368
  38.6 430.5 %all-gather.19.cloned.1.call-start = ((), (), s32[]{:S(2)}) async-start(), calls=%async_computation.3 | async-start | bytes 6635520 | tf_op jit(solution)/shard_map/all_gather | solution.py:369
  39.1 429.9 %all-gather.27.cloned.1.call-start = ((), (), s32[]{:S(2)}) async-start(), calls=%async_computation.7 | async-start | bytes 5242880 | tf_op jit(solution)/shard_map/all_gather | solution.py:395
  304.5 309.4 %all-gather.23.cloned.1.call-start = ((), (), s32[]{:S(2)}) async-start(), calls=%async_computation.5 | async-start | bytes 5242880 | tf_op jit(solution)/shard_map/all_gather | solution.py:395
Sparse Core Ops, SparseCore 0:
  11.6 60.3 all-gather.12
  73.5 31.4 all-gather.24
  106.9 37.8 all-gather.14
  146.2 31.4 all-gather.20
  179.4 57.9 all-gather.16
  239.0 37.8 all-gather.18
  304.7 31.3 all-gather.26
  455.3 31.3 all-gather.22
